TPU v7x, 32 devices: a whole 2x2x4 slice. The times are simulated.
32 devices in a mesh: group: 4 (over z), tensor: 8 (over y, x, core).
Axes of the slice: x: 2, y: 2, z: 4, core: 2. Of those that a mesh axis runs over, the one named last changes fastest.
Arguments:
- key_value_cache: bfloat16 [256, 1024, 256], P(('group', 'tensor')), may hold values from -8 to 8
- queries: bfloat16 [32, 48, 128], P('group'), may hold values from -200 to 200
- fresh_key_value: bfloat16 [32, 8, 256], P('group'), may hold values from -6 to 6
- lengths: int32 [32], P('group'), may hold values from 2 to 1023
- residual: bfloat16 [32, 6144], P('group'), may hold values from -100 to 100
- norm_gain: float32 [6144], replicated, may hold values from 0.1 to 1.9
- router_weight: bfloat16 [6144, 8], replicated, may hold values from -0.078125 to 0.078125
- routing: int32 [32, 2], P('group'), may hold values from 0 to 7, all different within a row
- expert_gate: bfloat16 [8, 6144, 8192], P(None, 'group', 'tensor'), may hold values from -0.078125 to 0.078125
- expert_up: bfloat16 [8, 6144, 8192], P(None, 'group', 'tensor'), may hold values from -0.078125 to 0.078125
Outputs:
- updated: bfloat16 [32, 6144], P('group')
- expert_hidden: bfloat16 [32, 2, 8192], P('group', None, 'tensor')
- new_cache: bfloat16 [32, 8, 1024, 256], P('group', None, 'tensor')
Inputs may be any that keep to these rules, and one draw needn't show every extreme that they name: Slot lengths[s] of sequence s receives its new token. `routing`: A token's two experts differ.
All inputs are finite; a program needn't handle non-finite values.
Results may differ from a plain program's by a relative error of at most 0.028.
Values may be sent and summed in bfloat16 or wider, within the bound.
No kernel may reach another device: no remote copies, remote signals or barrier semaphores. Data moves between devices by JAX's collectives and lax.ppermute only.
A program may use at most 128 MiB of HBM per device.

v0:
```python
import math
import jax
import jax.numpy as jnp
from jax import lax
from jax.sharding import PartitionSpec as P


def body(
    key_value_cache,
    queries,
    fresh_key_value,
    lengths,
    residual,
    norm_gain,
    router_weight,
    routing,
    expert_gate,
    expert_up,
):
    tensor_rank = lax.axis_index("tensor")
    seq_local = queries.shape[0]
    q_heads = queries.shape[1]
    kv_heads = fresh_key_value.shape[1]
    head_size = fresh_key_value.shape[2] // 2
    query_group_width = q_heads // kv_heads
    score_scale = 1.0 / math.sqrt(head_size)
    arrived = lax.all_to_all(key_value_cache, "tensor", split_axis=1, concat_axis=0, tiled=True)
    local_span = arrived.shape[1]
    arrived = arrived.reshape(seq_local, kv_heads, local_span, 2 * head_size)
    slot_index = tensor_rank * local_span + lax.broadcasted_iota(jnp.int32, (local_span,), 0)
    new_slot = slot_index[None, None, :, None] == lengths[:, None, None, None]
    new_cache = jnp.where(new_slot, fresh_key_value[:, :, None, :], arrived)
    pair_count = key_value_cache.shape[0]
    pair_begin = tensor_rank * pair_count
    query_vectors = lax.dynamic_slice_in_dim(
        queries.reshape(seq_local * kv_heads, query_group_width, head_size),
        pair_begin,
        pair_count,
        0,
    )
    own_rows = lax.dynamic_slice_in_dim(
        fresh_key_value.reshape(seq_local * kv_heads, 2 * head_size), pair_begin, pair_count, 0
    )
    every_length = jnp.broadcast_to(lengths[:, None], (seq_local, kv_heads)).reshape(
        seq_local * kv_heads
    )
    pair_length = lax.dynamic_slice_in_dim(every_length, pair_begin, pair_count, 0)
    scores = (
        jnp.einsum(
            "pgd,ptd->pgt",
            query_vectors,
            key_value_cache[..., :head_size],
            preferred_element_type=jnp.float32,
        )
        * score_scale
    )
    own_score = (
        jnp.einsum(
            "pgd,pd->pg", query_vectors, own_rows[:, :head_size], preferred_element_type=jnp.float32
        )
        * score_scale
    )
    visible = (
        lax.broadcasted_iota(jnp.int32, (1, 1, key_value_cache.shape[1]), 2)
        < pair_length[:, None, None]
    )
    peak = jnp.maximum(jnp.max(jnp.where(visible, scores, -1e30), -1), own_score)
    attention_weights = jnp.where(visible, jnp.exp(scores - peak[..., None]), 0.0)
    own_weight = jnp.exp(own_score - peak)
    denominator = jnp.sum(attention_weights, -1) + own_weight
    weighted = jnp.einsum(
        "pgt,ptd->pgd",
        attention_weights.astype(jnp.bfloat16),
        key_value_cache[..., head_size:],
        preferred_element_type=jnp.float32,
    )
    own_rounded = lax.optimization_barrier(own_weight.astype(jnp.bfloat16)).astype(jnp.float32)
    weighted = weighted + own_rounded[..., None] * own_rows[:, None, head_size:].astype(jnp.float32)
    head_result = (weighted / denominator[..., None]).reshape(
        pair_count, query_group_width * head_size
    )
    gathered = lax.all_gather(head_result, "tensor", axis=0, tiled=True)
    attention = gathered.reshape(seq_local, q_heads * head_size)
    updated = (residual.astype(jnp.float32) + attention).astype(jnp.bfloat16)
    stream = updated.astype(jnp.float32)
    normed = (
        stream * lax.rsqrt(jnp.mean(stream * stream, -1, keepdims=True) + 1e-05) * norm_gain
    ).astype(jnp.bfloat16)
    logits = jnp.dot(normed, router_weight, preferred_element_type=jnp.float32)
    expert_count = router_weight.shape[1]
    expert_ids = lax.broadcasted_iota(jnp.int32, (1, 1, expert_count), 2)
    chosen_mask = routing[:, :, None] == expert_ids
    chosen_logits = jnp.sum(jnp.where(chosen_mask, logits[:, None, :], 0.0), -1)
    gate_weights = jax.nn.sigmoid(chosen_logits - chosen_logits[:, ::-1])
    columns = lax.all_to_all(normed, "group", split_axis=1, concat_axis=0, tiled=True)
    gate_part = jnp.einsum("td,edf->tef", columns, expert_gate, preferred_element_type=jnp.float32)
    up_part = jnp.einsum("td,edf->tef", columns, expert_up, preferred_element_type=jnp.float32)
    summed = lax.psum_scatter(
        jnp.stack((gate_part, up_part), 2).astype(jnp.bfloat16),
        "group",
        scatter_dimension=0,
        tiled=True,
    ).astype(jnp.float32)
    picked = jnp.sum(jnp.where(chosen_mask[:, :, :, None, None], summed[:, None], 0.0), 2)
    expert_hidden = (
        gate_weights[:, :, None] * jax.nn.silu(picked[:, :, 0]) * picked[:, :, 1]
    ).astype(jnp.bfloat16)
    return (updated, expert_hidden, new_cache)


def solution(mesh):
    in_specs = (
        P(("group", "tensor"), None, None),
        P("group", None, None),
        P("group", None, None),
        P("group"),
        P("group", None),
        P(),
        P(),
        P("group", None),
        P(None, "group", "tensor"),
        P(None, "group", "tensor"),
    )
    out_specs = (P("group", None), P("group", None, "tensor"), P("group", None, "tensor", None))
    return jax.shard_map(body, mesh=mesh, in_specs=in_specs, out_specs=out_specs, check_vma=False)
```

profile of v0, /device:TPU:0, one launch (start us, length us, event | category | flops | bytes accessed | tf_op | source)
XLA Modules:
  0.0 109.6 jit_solution(10600744194444090793)
XLA Ops:
  7.2 0.0 copy-start
  7.2 0.0 copy-start.2
  7.2 0.0 copy-start.4
  7.2 0.8 broadcast_in_dim.87
  8.0 0.1 reshape.106
  8.1 0.1 dynamic_slice.9
  8.1 0.1 iota_compare_fusion
  8.2 0.9 reshape.107
  9.2 0.7 dynamic-slice_convert_fusion
  9.9 0.1 fusion.30
  10.0 2.3 %select_reduce_fusion.1 = (f32[8,6]{1,0:T(8,128)S(1)}, f32[8,6,1024]{2,1,0:T(8,128)S(1)}) fusion(pred[8,1024]{1,0:T(8,128)(4,1)S(1)} %iota_compare_fusion, bf16[8,1024,256]{2,1,0:T(8,128)(2,1)} %param.10, bf16[64,6,128]{2,1,0:T(8,128)(2,1)S(1)} %reshape.107, s32[]{:T(128)S(6)} %select_n.24), kind=kOutput, calls=%fused_computation.18 | convolution fusion | flops 12730320 | bytes 2318532 | tf_op jit(solution)/shard_map/pgd,ptd->pgt/dot_general | solution.py:49
  12.3 0.2 fusion.18
  12.6 2.0 %fusion.15 = f32[1,8,6,128]{3,2,1,0:T(8,128)S(1)} fusion(bf16[8,1024,256]{2,1,0:T(8,128)(2,1)} %param.10, f32[8,6,1024]{2,1,0:T(8,128)S(1)} %get-tuple-element.21, f32[8,6]{1,0:T(8,128)S(1)} %multiply_maximum_fusion, pred[8,1024]{1,0:T(8,128)(4,1)S(1)} %iota_compare_fusion, f32[8,6]{1,0:T(8,128)S(1)} %get-tuple-element.19, ...), kind=kOutput, calls=%fused_computation.12 | convolution fusion | flops 12748800 | bytes 2331200 | tf_op jit(solution)/shard_map/pgt,ptd->pgd/dot_general | solution.py:71
  14.6 10.7 %all_gather.3 = f32[64,768]{1,0:T(8,128)S(1)} all-gather(f32[8,768]{1,0:T(8,128)S(1)} %bitcast.58), channel_id=1, replica_groups=mesh['group'=4,'tensor'=8] {'tensor'}, dimensions={0}, use_global_device_ids=true | all-gather | bytes 221184 | tf_op jit(solution)/shard_map/all_gather | solution.py:82
  25.4 0.0 copy-done.2
  25.4 0.2 fusion.20
  25.6 0.0 copy-start.1
  25.6 0.0 copy-done.4
  25.6 0.7 fusion.22
  26.4 4.9 %all-to-all-start = ((bf16[8,4,1536]{2,0,1:T(8,128)(2,1)}), bf16[8,4,1536]{2,0,1:T(8,128)(2,1)S(1)}, u32[]{:S(2)}, u32[]{:S(2)}) async-start(bf16[8,4,1536]{2,0,1:T(8,128)(2,1)} %bitcast.4), calls=%async_computation | async-start | bytes 196608 | tf_op jit(solution)/shard_map/all_to_all | solution.py:95
  31.2 6.6 %copy.30 = bf16[8,1024,256]{2,0,1:T(8,128)(2,1)} copy(bf16[8,1024,256]{2,1,0:T(8,128)(2,1)} %param.10) | data formatting | bytes 8388608 | tf_op args[0]
  37.8 0.0 copy-done.1
  37.8 0.0 all-to-all-done
  37.8 4.5 %all-to-all-start.1 = ((bf16[8,1024,256]{2,0,1:T(8,128)(2,1)}), bf16[8,1024,256]{2,0,1:T(8,128)(2,1)}, u32[]{:S(2)}, u32[]{:S(2)}) async-start(bf16[8,1024,256]{2,0,1:T(8,128)(2,1)} %copy.30), calls=%async_computation.1 | async-start | bytes 8388608 | tf_op jit(solution)/shard_map/all_to_all | solution.py:27
  42.3 0.0 reduce-scatter.4.cloned.1.call-start
  42.4 10.6 %fusion.4 = bf16[32,8,1,1024]{3,0,1,2:T(8,128)(2,1)S(1)} fusion(bf16[8,1536,1024]{2,1,0:T(8,128)(2,1)} %param.18, bf16[8,4,1536]{2,0,1:T(8,128)(2,1)S(1)} %all-to-all-done), kind=kOutput, calls=%fused_computation.7 | convolution fusion | flops 805568512 | bytes 25788416 | tf_op jit(solution)/shard_map/td,edf->tef/dot_general | solution.py:96
  53.0 10.6 %fusion.5 = bf16[32,8,1,1024]{3,0,1,2:T(8,128)(2,1)S(1)} fusion(bf16[8,1536,1024]{2,1,0:T(8,128)(2,1)} %param.19, bf16[8,4,1536]{2,0,1:T(8,128)(2,1)S(1)} %all-to-all-done), kind=kOutput, calls=%fused_computation.8 | convolution fusion | flops 805568512 | bytes 25788416 | tf_op jit(solution)/shard_map/td,edf->tef/dot_general | solution.py:97
  63.6 0.0 copy-start.3
  63.6 0.0 copy-start.5
  63.6 0.0 copy-start.6
  63.6 0.1 pad_maximum_fusion
  63.7 1.1 copy.40
  64.8 0.0 reduce-scatter.4.cloned.1.call-update
  64.8 0.0 copy-done.3
  64.8 0.0 copy-done.5
  64.8 0.1 iota_compare_fusion.1
  64.9 0.0 copy-done
  64.9 1.1 fusion.40
  66.0 0.2 select_reduce_fusion.2
  66.2 0.1 copy.25
  66.3 0.0 copy-done.6
  66.3 0.1 broadcast_compare_fusion
  66.3 27.7 %reduce-scatter.4.cloned.1.call-done = bf16[8,16384]{1,0:T(8,128)(2,1)} async-done(((bf16[32,16384]{1,0:T(8,128)(2,1)}), bf16[8,16384]{1,0:T(8,128)(2,1)}) %reduce-scatter.4.cloned.1.call-update) | async-done | bytes 262160
  94.0 1.1 %copy.52 = bf16[1,8,16,1024]{3,2,1,0:T(8,128)(2,1)S(1)} copy(bf16[1,8,16,1024]{3,1,2,0:T(8,128)(2,1)} %bitcast.57) | data formatting | bytes 524288
  95.1 0.2 copy_convert_fusion
  95.3 0.3 copy.27
  95.6 0.4 select_reduce_fusion
  96.0 0.1 fusion.39
  96.1 0.7 fusion.29
  96.8 0.0 all-to-all-done.1
  96.8 3.1 %copy.31 = bf16[8,1024,256]{2,1,0:T(8,128)(2,1)S(1)} copy(bf16[8,1024,256]{2,0,1:T(8,128)(2,1)} %all-to-all-done.1) | data formatting | bytes 8388608 | tf_op jit(solution)/shard_map/all_to_all | solution.py:27
  99.9 0.4 broadcast_select_fusion
  100.3 2.5 %copy.32 = bf16[8,8,128,256]{3,2,1,0:T(8,128)(2,1)} copy(bf16[8,8,128,256]{3,2,0,1:T(8,128)(2,1)S(1)} %broadcast_select_fusion) | data formatting | bytes 8388608
  (11 shorter events, 0.1 us)
Async XLA Ops:
  7.2 57.7 %copy-start = (bf16[6144,8]{0,1:T(8,128)(2,1)S(1)}, bf16[6144,8]{0,1:T(8,128)(2,1)}, u32[]{:S(2)}) copy-start(bf16[6144,8]{0,1:T(8,128)(2,1)} %param.16) | copy-start | bytes 294916
  7.2 18.2 %copy-start.2 = (bf16[8,6144]{1,0:T(8,128)(2,1)S(1)}, bf16[8,6144]{1,0:T(8,128)(2,1)}, u32[]{:S(2)}) copy-start(bf16[8,6144]{1,0:T(8,128)(2,1)} %param.14) | copy-start | bytes 294916
  7.2 18.4 %copy-start.4 = (f32[6144]{0:T(1024)S(1)}, f32[6144]{0:T(1024)}, u32[]{:S(2)}) copy-start(f32[6144]{0:T(1024)} %param.15) | copy-start | bytes 73732
  25.6 12.2 %copy-start.1 = (bf16[8,6144]{1,0:T(8,128)(2,1)}, bf16[8,6144]{1,0:T(8,128)(2,1)S(1)}, u32[]{:S(2)}) copy-start(bf16[8,6144]{1,0:T(8,128)(2,1)S(1)} %get-tuple-element.13) | copy-start | bytes 294916
  26.4 11.4 %all-to-all-start = ((bf16[8,4,1536]{2,0,1:T(8,128)(2,1)}), bf16[8,4,1536]{2,0,1:T(8,128)(2,1)S(1)}, u32[]{:S(2)}, u32[]{:S(2)}) async-start(bf16[8,4,1536]{2,0,1:T(8,128)(2,1)} %bitcast.4), calls=%async_computation | async-start | bytes 196608 | tf_op jit(solution)/shard_map/all_to_all | solution.py:95
  37.8 59.0 %all-to-all-start.1 = ((bf16[8,1024,256]{2,0,1:T(8,128)(2,1)}), bf16[8,1024,256]{2,0,1:T(8,128)(2,1)}, u32[]{:S(2)}, u32[]{:S(2)}) async-start(bf16[8,1024,256]{2,0,1:T(8,128)(2,1)} %copy.30), calls=%async_computation.1 | async-start | bytes 8388608 | tf_op jit(solution)/shard_map/all_to_all | solution.py:27
  42.3 51.7 %reduce-scatter.4.cloned.1.call-start = ((), (), s32[]{:S(2)}) async-start(), calls=%async_computation.3 | async-start | bytes 1310720
  63.6 1.2 %copy-start.3 = (bf16[8,8,256]{2,1,0:T(8,128)(2,1)S(1)}, bf16[8,8,256]{2,1,0:T(8,128)(2,1)}, u32[]{:S(2)}) copy-start(bf16[8,8,256]{2,1,0:T(8,128)(2,1)} %param.12) | copy-start | bytes 98308
  63.6 1.2 %copy-start.5 = (s32[8,2]{0,1:T(2,128)S(1)}, s32[8,2]{0,1:T(2,128)}, u32[]{:S(2)}) copy-start(s32[8,2]{0,1:T(2,128)} %param.17) | copy-start | bytes 196
  63.6 2.7 %copy-start.6 = (s32[8]{0:T(128)S(1)}, s32[8]{0:T(128)}, u32[]{:S(2)}) copy-start(s32[8]{0:T(128)} %param.13) | copy-start | bytes 100
Sparse Core Ops, SparseCore 0:
  64.9 29.0 reduce-scatter.3
where the time goes:
time: 110 us
  waiting for transfers between devices  27.7 us (25%)
  matrix products  26.7 us (24%)
  local copies, waits for them, and re-layouts  16.8 us (15%)
  between operations  14.2 us (13%)
  blocking collectives  10.7 us (10%)
  starting transfers between devices  9.45 us (9%)
  other arithmetic  4.03 us (4%)
    unnamed x2, waiting for transfers between devices  27.7 us
    unnamed x20, local copies, waits for them, and re-layouts  11.3 us
    all_gather x1, blocking collectives, body(): gathered = lax.all_gather(head_result, 'tensor', axis=0, tiled=True)  10.7 us
    dot_general x1, matrix products, body(): jnp.einsum('td,edf->tef', columns, expert_gate, preferred_element_type=jn...  10.6 us
    dot_general x1, matrix products, body(): jnp.einsum('td,edf->tef', columns, expert_up, preferred_element_type=jnp....  10.6 us
    all_to_all x1, starting transfers between devices, body(): lax.all_to_all(normed, 'group', split_axis=1, concat_axis=0, tiled=True)  4.87 us
    all_to_all x1, starting transfers between devices, body(): lax.all_to_all(key_value_cache, 'tensor', split_axis=1, concat_axis=0, ti...  4.54 us
    all_to_all x1, local copies, waits for them, and re-layouts, body(): lax.all_to_all(key_value_cache, 'tensor', split_axis=1, concat_axis=0, ti...  3.05 us
  transfers between devices with their start and end apart: 3, of which 1 were waited for; matrix products, arithmetic and copies ran while one was open for 30% of the time, Pallas kernels for 0%

commit v1 on v0

--- a/solution.py
+++ b/solution.py
@@ -79,7 +79,9 @@
     head_result = (weighted / denominator[..., None]).reshape(
         pair_count, query_group_width * head_size
     )
-    gathered = lax.all_gather(head_result, "tensor", axis=0, tiled=True)
+    gathered = jnp.concatenate(
+        lax.all_to_all(jnp.stack([head_result] * lax.axis_size("tensor")), "tensor", 0, 0), axis=0
+    )
     attention = gathered.reshape(seq_local, q_heads * head_size)
     updated = (residual.astype(jnp.float32) + attention).astype(jnp.bfloat16)
     stream = updated.astype(jnp.float32)

time: 110 us -> 111 us (level)
    all_to_all x0 -> x1, blocking collectives: none -> 11.2 us  [body(): lax.all_to_all(jnp.stack([head_result] * lax.axis_size('tensor')), 'tenso...]
    all_gather x1 -> x0, blocking collectives: 10.7 us -> none  [body(): gathered = lax.all_gather(head_result, 'tensor', axis=0, tiled=True)]
    unnamed x20 -> x21, local copies, waits for them, and re-layouts: 11.3 us -> 11.4 us
where the time goes in v1:
time: 111 us; the launch traced here: 110 us
  waiting for transfers between devices  27.7 us (25%)
  matrix products  26.7 us (24%)
  local copies, waits for them, and re-layouts  16.8 us (15%)
  between operations  14.3 us (13%)
  blocking collectives  11.2 us (10%)
  starting transfers between devices  9.45 us (9%)
  other arithmetic  4.04 us (4%)
    unnamed x2, waiting for transfers between devices  27.7 us
    unnamed x21, local copies, waits for them, and re-layouts  11.4 us
    all_to_all x1, blocking collectives, body(): lax.all_to_all(jnp.stack([head_result] * lax.axis_size('tensor')), 'tenso...  11.2 us
    dot_general x1, matrix products, body(): jnp.einsum('td,edf->tef', columns, expert_gate, preferred_element_type=jn...  10.6 us
    dot_general x1, matrix products, body(): jnp.einsum('td,edf->tef', columns, expert_up, preferred_element_type=jnp....  10.6 us
    all_to_all x1, starting transfers between devices, body(): lax.all_to_all(normed, 'group', split_axis=1, concat_axis=0, tiled=True)  4.87 us
    all_to_all x1, starting transfers between devices, body(): lax.all_to_all(key_value_cache, 'tensor', split_axis=1, concat_axis=0, ti...  4.54 us
    all_to_all x1, local copies, waits for them, and re-layouts, body(): lax.all_to_all(key_value_cache, 'tensor', split_axis=1, concat_axis=0, ti...  3.05 us
  transfers between devices with their start and end apart: 3, of which 1 were waited for; matrix products, arithmetic and copies ran while one was open for 30% of the time, Pallas kernels for 0%

profile of v1, /device:TPU:0, one launch (start us, length us, event | category | flops | bytes accessed | tf_op | source)
XLA Modules:
  0.0 110.2 jit_solution(12860447726771310441)
XLA Ops:
  7.2 0.0 copy-start
  7.2 0.0 copy-start.2
  7.2 0.0 copy-start.4
  7.2 0.8 broadcast_in_dim.87
  8.0 0.1 reshape.102
  8.1 0.1 dynamic_slice.9
  8.1 0.1 iota_compare_fusion
  8.2 0.9 reshape.103
  9.2 0.7 dynamic-slice_convert_fusion
  9.9 0.1 fusion.30
  10.0 2.3 %select_reduce_fusion.1 = (f32[8,6]{1,0:T(8,128)S(1)}, f32[8,6,1024]{2,1,0:T(8,128)S(1)}) fusion(pred[8,1024]{1,0:T(8,128)(4,1)S(1)} %iota_compare_fusion, bf16[8,1024,256]{2,1,0:T(8,128)(2,1)} %param.10, bf16[64,6,128]{2,1,0:T(8,128)(2,1)S(1)} %reshape.103, s32[]{:T(128)S(6)} %select_n.24), kind=kOutput, calls=%fused_computation.18 | convolution fusion | flops 12730320 | bytes 2318532 | tf_op jit(solution)/shard_map/pgd,ptd->pgt/dot_general | solution.py:49
  12.3 0.2 fusion.18
  12.6 2.0 %fusion.15 = f32[1,8,6,128]{3,2,1,0:T(8,128)S(1)} fusion(bf16[8,1024,256]{2,1,0:T(8,128)(2,1)} %param.10, f32[8,6,1024]{2,1,0:T(8,128)S(1)} %get-tuple-element.21, f32[8,6]{1,0:T(8,128)S(1)} %multiply_maximum_fusion, pred[8,1024]{1,0:T(8,128)(4,1)S(1)} %iota_compare_fusion, f32[8,6]{1,0:T(8,128)S(1)} %get-tuple-element.19, ...), kind=kOutput, calls=%fused_computation.12 | convolution fusion | flops 12748800 | bytes 2331200 | tf_op jit(solution)/shard_map/pgt,ptd->pgd/dot_general | solution.py:71
  14.6 11.2 %all_to_all.39 = f32[8,8,768]{2,1,0:T(8,128)S(1)} all-to-all(f32[8,8,768]{2,1,0:T(8,128)S(1)} %stack.15), channel_id=1, replica_groups=mesh['group'=4,'tensor'=8] {'tensor'}, dimensions={0} | all-to-all | bytes 393216 | tf_op jit(solution)/shard_map/all_to_all | solution.py:83
  25.8 0.1 copy.40
  25.9 0.0 copy-done.2
  25.9 0.2 fusion.20
  26.1 0.0 copy-start.1
  26.1 0.0 copy-done.4
  26.1 0.7 fusion.22
  26.9 4.9 %all-to-all-start.1 = ((bf16[8,4,1536]{2,0,1:T(8,128)(2,1)}), bf16[8,4,1536]{2,0,1:T(8,128)(2,1)S(1)}, u32[]{:S(2)}, u32[]{:S(2)}) async-start(bf16[8,4,1536]{2,0,1:T(8,128)(2,1)} %bitcast.4), calls=%async_computation.1 | async-start | bytes 196608 | tf_op jit(solution)/shard_map/all_to_all | solution.py:97
  31.7 6.6 %copy.30 = bf16[8,1024,256]{2,0,1:T(8,128)(2,1)} copy(bf16[8,1024,256]{2,1,0:T(8,128)(2,1)} %param.10) | data formatting | bytes 8388608 | tf_op args[0]
  38.3 0.0 copy-done.1
  38.3 0.0 all-to-all-done.1
  38.3 4.5 %all-to-all-start.2 = ((bf16[8,1024,256]{2,0,1:T(8,128)(2,1)}), bf16[8,1024,256]{2,0,1:T(8,128)(2,1)}, u32[]{:S(2)}, u32[]{:S(2)}) async-start(bf16[8,1024,256]{2,0,1:T(8,128)(2,1)} %copy.30), calls=%async_computation.2 | async-start | bytes 8388608 | tf_op jit(solution)/shard_map/all_to_all | solution.py:27
  42.9 0.0 reduce-scatter.4.cloned.1.call-start
  42.9 10.6 %fusion.4 = bf16[32,8,1,1024]{3,0,1,2:T(8,128)(2,1)S(1)} fusion(bf16[8,1536,1024]{2,1,0:T(8,128)(2,1)} %param.18, bf16[8,4,1536]{2,0,1:T(8,128)(2,1)S(1)} %all-to-all-done.1), kind=kOutput, calls=%fused_computation.7 | convolution fusion | flops 805568512 | bytes 25788416 | tf_op jit(solution)/shard_map/td,edf->tef/dot_general | solution.py:98
  53.5 10.6 %fusion.5 = bf16[32,8,1,1024]{3,0,1,2:T(8,128)(2,1)S(1)} fusion(bf16[8,1536,1024]{2,1,0:T(8,128)(2,1)} %param.19, bf16[8,4,1536]{2,0,1:T(8,128)(2,1)S(1)} %all-to-all-done.1), kind=kOutput, calls=%fused_computation.8 | convolution fusion | flops 805568512 | bytes 25788416 | tf_op jit(solution)/shard_map/td,edf->tef/dot_general | solution.py:99
  64.1 0.0 copy-start.3
  64.1 0.0 copy-start.5
  64.1 0.0 copy-start.6
  64.1 0.1 pad_maximum_fusion
  64.2 1.1 copy.41
  65.3 0.0 reduce-scatter.4.cloned.1.call-update
  65.3 0.0 copy-done.3
  65.3 0.0 copy-done.5
  65.3 0.1 iota_compare_fusion.1
  65.4 0.0 copy-done.6
  65.4 0.1 broadcast_compare_fusion
  65.5 0.0 copy-done
  65.5 1.1 fusion.40
  66.6 0.2 select_reduce_fusion.2
  66.8 0.1 copy.25
  66.8 27.7 %reduce-scatter.4.cloned.1.call-done = bf16[8,16384]{1,0:T(8,128)(2,1)} async-done(((bf16[32,16384]{1,0:T(8,128)(2,1)}), bf16[8,16384]{1,0:T(8,128)(2,1)}) %reduce-scatter.4.cloned.1.call-update) | async-done | bytes 262160
  94.5 1.1 copy.53
  95.6 0.2 copy_convert_fusion
  95.8 0.3 copy.27
  96.1 0.4 select_reduce_fusion
  96.5 0.1 fusion.39
  96.6 0.7 fusion.29
  97.4 0.0 all-to-all-done.2
  97.4 3.1 %copy.31 = bf16[8,1024,256]{2,1,0:T(8,128)(2,1)S(1)} copy(bf16[8,1024,256]{2,0,1:T(8,128)(2,1)} %all-to-all-done.2) | data formatting | bytes 8388608 | tf_op jit(solution)/shard_map/all_to_all | solution.py:27
  100.4 0.4 broadcast_select_fusion
  100.8 2.5 %copy.32 = bf16[8,8,128,256]{3,2,1,0:T(8,128)(2,1)} copy(bf16[8,8,128,256]{3,2,0,1:T(8,128)(2,1)S(1)} %broadcast_select_fusion) | data formatting | bytes 8388608
  (11 shorter events, 0.1 us)
Async XLA Ops:
  7.2 58.3 %copy-start = (bf16[6144,8]{0,1:T(8,128)(2,1)S(1)}, bf16[6144,8]{0,1:T(8,128)(2,1)}, u32[]{:S(2)}) copy-start(bf16[6144,8]{0,1:T(8,128)(2,1)} %param.16) | copy-start | bytes 294916
  7.2 18.7 %copy-start.2 = (bf16[8,6144]{1,0:T(8,128)(2,1)S(1)}, bf16[8,6144]{1,0:T(8,128)(2,1)}, u32[]{:S(2)}) copy-start(bf16[8,6144]{1,0:T(8,128)(2,1)} %param.14) | copy-start | bytes 294916
  7.2 18.9 %copy-start.4 = (f32[6144]{0:T(1024)S(1)}, f32[6144]{0:T(1024)}, u32[]{:S(2)}) copy-start(f32[6144]{0:T(1024)} %param.15) | copy-start | bytes 73732
  26.1 12.2 %copy-start.1 = (bf16[8,6144]{1,0:T(8,128)(2,1)}, bf16[8,6144]{1,0:T(8,128)(2,1)S(1)}, u32[]{:S(2)}) copy-start(bf16[8,6144]{1,0:T(8,128)(2,1)S(1)} %get-tuple-element.13) | copy-start | bytes 294916
  26.9 11.4 %all-to-all-start.1 = ((bf16[8,4,1536]{2,0,1:T(8,128)(2,1)}), bf16[8,4,1536]{2,0,1:T(8,128)(2,1)S(1)}, u32[]{:S(2)}, u32[]{:S(2)}) async-start(bf16[8,4,1536]{2,0,1:T(8,128)(2,1)} %bitcast.4), calls=%async_computation.1 | async-start | bytes 196608 | tf_op jit(solution)/shard_map/all_to_all | solution.py:97
  38.3 59.0 %all-to-all-start.2 = ((bf16[8,1024,256]{2,0,1:T(8,128)(2,1)}), bf16[8,1024,256]{2,0,1:T(8,128)(2,1)}, u32[]{:S(2)}, u32[]{:S(2)}) async-start(bf16[8,1024,256]{2,0,1:T(8,128)(2,1)} %copy.30), calls=%async_computation.2 | async-start | bytes 8388608 | tf_op jit(solution)/shard_map/all_to_all | solution.py:27
  42.9 51.7 %reduce-scatter.4.cloned.1.call-start = ((), (), s32[]{:S(2)}) async-start(), calls=%async_computation.4 | async-start | bytes 1310720
  64.1 1.2 %copy-start.3 = (bf16[8,8,256]{2,1,0:T(8,128)(2,1)S(1)}, bf16[8,8,256]{2,1,0:T(8,128)(2,1)}, u32[]{:S(2)}) copy-start(bf16[8,8,256]{2,1,0:T(8,128)(2,1)} %param.12) | copy-start | bytes 98308
  64.1 1.2 %copy-start.5 = (s32[8,2]{0,1:T(2,128)S(1)}, s32[8,2]{0,1:T(2,128)}, u32[]{:S(2)}) copy-start(s32[8,2]{0,1:T(2,128)} %param.17) | copy-start | bytes 196
  64.1 1.3 %copy-start.6 = (s32[8]{0:T(128)S(1)}, s32[8]{0:T(128)}, u32[]{:S(2)}) copy-start(s32[8]{0:T(128)} %param.13) | copy-start | bytes 100
Sparse Core Ops, SparseCore 0:
  65.4 29.0 reduce-scatter.3
